TPU v7x, 8 devices: a whole 2x2x1 slice. The times are simulated.
8 devices in a mesh: a3: 2 (over z, y), a2: 2 (over x), a1: 2 (over core).
Axes of the slice: x: 2, y: 2, z: 1, core: 2. Of those that a mesh axis runs over, the one named last changes fastest.
Arguments:
- tensor: bfloat16 [384, 720, 1440], P('a1', 'a2', 'a3')
- u_time: float32 [384, 48], replicated
- u_height: float32 [720, 88], replicated
- u_width: float32 [1440, 176], replicated
Outputs:
- output 1: float32 [384, 48], replicated
- output 2: float32 [720, 88], replicated
- output 3: float32 [1440, 176], replicated
- output 4: float32 [48, 88, 176], P('a1', 'a2', 'a3')
- output 5: float32 [], replicated
All inputs are finite; a program needn't handle non-finite values.
Results may differ from a plain program's by a relative error of at most 0.00743457.
Values are sent between devices in bfloat16 or wider.
A program may use at most 1 GiB of HBM per device.

v0:
```python
import jax
import jax.numpy as jnp
from jax import lax
from jax.sharding import PartitionSpec as P


def rows_of(factor, axis_name, count):
    start_row = lax.axis_index(axis_name) * count
    return lax.dynamic_slice_in_dim(factor, start_row, count, 0).astype(jnp.bfloat16)


def gram_update(local_rows, row_axes, sum_axes, factor):
    all_rows = lax.all_gather(local_rows, row_axes, axis=0, tiled=True)
    gram_part = lax.dot_general(local_rows, all_rows, (((1,), (1,)), ((), ())), preferred_element_type=jnp.float32)
    gram_rows = lax.psum(gram_part, sum_axes).astype(jnp.bfloat16)
    power_cols = jnp.dot(gram_rows, factor.astype(jnp.bfloat16), preferred_element_type=jnp.float32)
    col_sq = lax.psum(jnp.sum(power_cols * power_cols, axis=0, keepdims=True), row_axes)
    return lax.all_gather(power_cols / jnp.sqrt(col_sq), row_axes, axis=0, tiled=True)


def solution(mesh):
    def local_sweep(tensor, u_time, u_height, u_width):
        frames, grid_h, grid_w = tensor.shape
        t_part = jnp.dot(tensor.reshape(frames * grid_h, grid_w), rows_of(u_width, 'a3', grid_w), preferred_element_type=jnp.float32)
        t_mat = lax.psum_scatter(t_part.reshape(frames, grid_h, -1), 'a3', scatter_dimension=2, tiled=True).astype(jnp.bfloat16)
        y1_part = jnp.einsum('ihc,hb->icb', t_mat, rows_of(u_height, 'a2', grid_h), preferred_element_type=jnp.float32)
        y_one = lax.psum_scatter(y1_part, 'a2', scatter_dimension=2, tiled=True).astype(jnp.bfloat16)
        new_time = gram_update(y_one.reshape(frames, -1), 'a1', ('a2', 'a3'), u_time)
        time_rows = rows_of(new_time, 'a1', frames)
        y2_part = jnp.einsum('ihc,ia->hca', t_mat, time_rows, preferred_element_type=jnp.float32)
        y_two = lax.psum_scatter(y2_part, 'a1', scatter_dimension=2, tiled=True).astype(jnp.bfloat16)
        new_height = gram_update(y_two.reshape(grid_h, -1), 'a2', ('a1', 'a3'), u_height)
        z_part = lax.dot_general(time_rows, tensor.reshape(frames, grid_h * grid_w), (((0,), (0,)), ((), ())), preferred_element_type=jnp.float32)
        z_mat = lax.psum_scatter(z_part, 'a1', scatter_dimension=0, tiled=True).astype(jnp.bfloat16).reshape(-1, grid_h, grid_w)
        y3_part = jnp.einsum('ahw,hb->wab', z_mat, rows_of(new_height, 'a2', grid_h), preferred_element_type=jnp.float32)
        y_three = lax.psum_scatter(y3_part, 'a2', scatter_dimension=2, tiled=True).astype(jnp.bfloat16)
        new_width = gram_update(y_three.reshape(grid_w, -1), 'a3', ('a1', 'a2'), u_width)
        core_part = jnp.einsum('wab,wc->abc', y_three, rows_of(new_width, 'a3', grid_w), preferred_element_type=jnp.float32)
        core_tensor = lax.psum_scatter(core_part, 'a3', scatter_dimension=2, tiled=True)
        core_energy = lax.psum(jnp.sum(core_tensor * core_tensor), ('a1', 'a2', 'a3'))
        return new_time, new_height, new_width, core_tensor, core_energy

    return jax.shard_map(local_sweep, mesh=mesh, in_specs=(P('a1', 'a2', 'a3'), P(), P(), P()), out_specs=(P(), P(), P(), P('a1', 'a2', 'a3'), P()), check_vma=False)
```

profile of v0, /device:TPU:0, one launch (start us, length us, event | category | flops | bytes accessed | tf_op | source)
XLA Modules:
  0.0 2038.0 jit_solution(15734637894612104775)
XLA Ops:
  7.2 60.4 %convolution_bitcast_fusion = f32[69120,176]{0,1:T(8,128)} fusion(bf16[69120,720]{1,0:T(8,128)(2,1)} %bitcast, f32[1440,176]{0,1:T(8,128)} %param.7, s32[]{:T(128)S(6)} %select_n.11), kind=kOutput, calls=%fused_computation | convolution fusion | flops 17517772800 | bytes 155099136 | tf_op jit(solution)/shard_map/dot_general | solution.py:24
  67.6 60.5 %reshape.32 = f32[192,360,176]{1,0,2:T(8,128)} reshape(f32[69120,176]{0,1:T(8,128)} %convolution_bitcast_fusion) | data formatting | bytes 97320960 | tf_op jit(solution)/shard_map/reshape | solution.py:25
  128.1 66.2 %copy.37 = f32[192,360,176]{0,2,1:T(8,128)} copy(f32[192,360,176]{1,0,2:T(8,128)} %reshape.32) | data formatting | bytes 97320960 | tf_op jit(solution)/shard_map/reshape | solution.py:25
  194.4 704.8 %reduce-scatter.6.cloned.1.call-done = f32[192,360,88]{0,2,1:T(8,128)} async-done(((f32[192,360,176]{0,2,1:T(8,128)}), f32[192,360,88]{0,2,1:T(8,128)}) %reduce-scatter.6.cloned.1.call-update) | async-done | bytes 24330256 | tf_op jit(solution)/shard_map/reduce_scatter | solution.py:25
  899.2 16.7 convert_element_type.49
  916.0 23.5 %copy.38 = bf16[192,360,88]{1,2,0:T(8,128)(2,1)} copy(bf16[192,360,88]{0,2,1:T(8,128)(2,1)} %convert_element_type.49) | data formatting | bytes 24330240 | tf_op jit(solution)/shard_map/convert_element_type | solution.py:25
  939.4 14.7 fusion.12
  954.1 10.2 copy.39
  964.7 91.3 %reduce-scatter.8.cloned.1.call-done = f32[192,88,44]{0,1,2:T(8,128)} async-done(((f32[192,88,88]{0,1,2:T(8,128)}), f32[192,88,44]{0,1,2:T(8,128)}) %reduce-scatter.8.cloned.1.call-update) | async-done | bytes 2973712 | tf_op jit(solution)/shard_map/reduce_scatter | solution.py:27
  1065.8 229.8 %reshape.35 = bf16[192,259200]{1,0:T(8,128)(2,1)} reshape(bf16[192,360,720]{2,1,0:T(8,128)(2,1)} %param.4) | data formatting | bytes 199065600 | tf_op jit(solution)/shard_map/reshape | solution.py:33
  1300.1 20.4 all-reduce.9
  1325.4 11.5 fusion.17
  1337.0 8.8 copy.43
  1345.8 9.8 all-gather.10.cloned.1.call-start
  1355.6 48.6 %fusion.19 = f32[48,259200]{1,0:T(8,128)} fusion(bf16[192,259200]{1,0:T(8,128)(2,1)} %reshape.35, f32[384,48]{0,1:T(8,128)S(1)} %reshape.39, s32[]{:T(128)S(6)} %select_n.13), kind=kOutput, calls=%fused_computation.31 | convolution fusion | flops 4777574400 | bytes 149323776 | tf_op jit(solution)/shard_map/dot_general | solution.py:33
  1404.2 130.0 %all-reduce.11 = bf16[48,259200]{1,0:T(8,128)(2,1)} all-reduce(f32[48,259200]{1,0:T(8,128)} %fusion.19), channel_id=5, replica_groups=mesh['a3'=2,'a2'=2,'a1'=2] {'a1'}, use_global_device_ids=true, to_apply=%region_9.0.clone | all-reduce | flops 12441600 | bytes 74649600
  1539.3 10.4 dynamic-slice_convert_fusion
  1549.7 35.5 %reshape.36 = bf16[24,360,720]{2,1,0:T(8,128)(2,1)} reshape(bf16[24,259200]{1,0:T(8,128)(2,1)} %dynamic-slice_convert_fusion) | data formatting | bytes 24883200 | tf_op jit(solution)/shard_map/reshape | solution.py:34
  1588.7 42.0 %all-reduce.10 = bf16[360,720]{1,0:T(8,128)(2,1)S(1)} all-reduce(f32[360,720]{1,0:T(8,128)S(1)} %fusion.28), channel_id=1, replica_groups=mesh['a3'=2,'a2'=2,'a1'=2] {'a1','a3'}, use_global_device_ids=true, to_apply=%region_6.0 | all-reduce | flops 259200 | bytes 1555200 | tf_op jit(solution)/shard_map/psum | solution.py:15
  1631.1 4.9 psum.52
  1636.2 5.9 all-gather.1
  1642.4 6.3 convolution_bitcast_fusion.1
  1648.7 4.7 copy.46
  1653.5 77.2 %reduce-scatter.12.cloned.1.call-done = f32[720,24,44]{0,1,2:T(8,128)} async-done(((f32[720,24,88]{0,1,2:T(8,128)}), f32[720,24,44]{0,1,2:T(8,128)}) %reduce-scatter.12.cloned.1.call-update) | async-done | bytes 3041296 | tf_op jit(solution)/shard_map/reduce_scatter | solution.py:36
  1738.5 41.4 %all-gather.12.cloned.1.call-done = bf16[2,720,1056]{1,2,0:T(8,128)(2,1)} async-done(((bf16[1,720,1056]{1,2,0:T(8,128)(2,1)}), bf16[2,720,1056]{1,2,0:T(8,128)(2,1)}) %all-gather.12.cloned.1.call-update) | async-done | bytes 3041296 | tf_op jit(solution)/shard_map/all_gather | solution.py:13
  1779.8 4.3 copy.49
  1784.1 6.2 fusion.29
  1790.3 152.4 %all-reduce.12 = bf16[720,1440]{1,0:T(8,128)(2,1)S(1)} all-reduce(f32[720,1440]{1,0:T(8,128)} %fusion.29), channel_id=1, replica_groups=mesh['a3'=2,'a2'=2,'a1'=2] {'a1','a2'}, use_global_device_ids=true, to_apply=%region_11.0 | all-reduce | flops 1036800 | bytes 6220800 | tf_op jit(solution)/shard_map/psum | solution.py:15
  1944.9 4.9 psum.54
  1949.9 13.3 all-gather.3
  1970.2 35.1 %all-reduce.8.cloned.1.call-done = f32[24,44,176]{2,1,0:T(8,128)} async-done(((f32[24,44,176]{2,1,0:T(8,128)}), f32[24,44,176]{2,1,0:T(8,128)}) %all-reduce.8.cloned.1.call-update) | async-done | bytes 743440
  2008.4 22.4 %psum.55 = f32[]{:T(128)} all-reduce(f32[]{:T(128)} %get-tuple-element.25), channel_id=1, replica_groups=mesh['a3'=2,'a2'=2,'a1'=2] {'a1','a2','a3'}, use_global_device_ids=true, to_apply=%region_16.0 | all-reduce | flops 1 | bytes 8 | tf_op jit(solution)/shard_map/psum | solution.py:40
  (68 shorter events, 47.7 us)
Async XLA Ops:
  7.2 892.1 %reduce-scatter.6.cloned.1.call-start = ((), (), s32[]{:S(2)}) async-start(), calls=%async_computation.4 | async-start | bytes 97320960 | tf_op jit(solution)/shard_map/reduce_scatter | solution.py:25
  194.3 861.7 %reduce-scatter.8.cloned.1.call-start = ((), (), s32[]{:S(2)}) async-start(), calls=%async_computation.5 | async-start | bytes 11894784 | tf_op jit(solution)/shard_map/reduce_scatter | solution.py:27
  964.4 332.5 %all-gather.8.cloned.1.call-start = ((), (), s32[]{:S(2)}) async-start(), calls=%async_computation.6 | async-start | bytes 4571136 | tf_op jit(solution)/shard_map/all_gather | solution.py:13
  1065.8 468.5 %reduce-scatter.10.cloned.1.call-start = ((), (), s32[]{:S(2)}) async-start(), calls=%async_computation.7 | async-start | bytes 9732096 | tf_op jit(solution)/shard_map/reduce_scatter | solution.py:31
  1065.8 229.8 %copy-start.7 = (u32[8]{0:T(128)S(1)}, u32[8]{0:T(128)}, u32[]{:S(2)}) copy-start(u32[8]{0:T(128)} %constant.26) | copy-start | bytes 100
  1295.6 24.9 %copy-start.5 = (f32[384,48]{0,1:T(8,128)S(1)}, f32[384,48]{0,1:T(8,128)}, u32[]{:S(2)}) copy-start(f32[384,48]{0,1:T(8,128)} %param.5) | copy-start | bytes 221188
  1325.4 30.2 %copy-start.4 = (f32[384,48]{0,1:T(8,128)}, f32[384,48]{0,1:T(8,128)S(1)}, u32[]{:S(2)}) copy-start(f32[384,48]{0,1:T(8,128)S(1)} %reshape.39) | copy-start | bytes 221188
  1345.8 239.5 %all-gather.10.cloned.1.call-start = ((), (), s32[]{:S(2)}) async-start(), calls=%async_computation.8 | async-start | bytes 4700160 | tf_op jit(solution)/shard_map/all_gather | solution.py:13
  1539.3 191.4 %reduce-scatter.12.cloned.1.call-start = ((), (), s32[]{:S(2)}) async-start(), calls=%async_computation.9 | async-start | bytes 9732096 | tf_op jit(solution)/shard_map/reduce_scatter | solution.py:36
  1585.2 45.5 %copy-start.2 = (f32[720,88]{0,1:T(8,128)S(1)}, f32[720,88]{0,1:T(8,128)}, u32[]{:S(2)}) copy-start(f32[720,88]{0,1:T(8,128)} %param.6) | copy-start | bytes 760324
  1642.4 6.3 copy-start.3
  1653.4 126.4 %all-gather.12.cloned.1.call-start = ((), (), s32[]{:S(2)}) async-start(), calls=%async_computation.10 | async-start | bytes 4866048 | tf_op jit(solution)/shard_map/all_gather | solution.py:13
  1732.7 1.2 copy-start
  1736.4 268.9 %all-reduce.8.cloned.1.call-start = ((), (), s32[]{:S(2)}) async-start(), calls=%async_computation.11 | async-start | bytes 2359296
  1949.9 16.1 copy-start.1
  1964.1 4.8 copy-start.6
Sparse Core Ops, SparseCore 0:
  194.4 704.7 reduce-scatter.5
  964.5 91.4 reduce-scatter.7
  1065.9 9.3 all-gather.7
  1345.9 9.8 reduce-scatter.9
  1539.4 41.4 all-gather.9
  1653.5 77.0 reduce-scatter.11
  1736.5 43.2 all-gather.11
  1969.1 36.2 all-reduce.7
where the time goes:
time: 2050 us; the launch traced here: 2040 us
  waiting for transfers between devices  950 us (46%)
  local copies, waits for them, and re-layouts  475 us (23%)
  blocking collectives  401 us (20%)
  matrix products  160 us (8%)
  other arithmetic  25.6 us (1%)
    reduce_scatter x1, waiting for transfers between devices, local_sweep(): lax.psum_scatter(t_part.reshape(frames, grid_h, -1), 'a3', scatter_dimens...  705 us
    reshape x1, local copies, waits for them, and re-layouts, local_sweep(): tensor.reshape(frames, grid_h * grid_w)  230 us
    psum x3, blocking collectives, gram_update(): gram_rows = lax.psum(gram_part, sum_axes).astype(jnp.bfloat16)  215 us
    unnamed x1, blocking collectives  130 us
    reshape x2, local copies, waits for them, and re-layouts, local_sweep(): t_part.reshape(frames, grid_h, -1)  127 us
    reduce_scatter x1, waiting for transfers between devices, local_sweep(): lax.psum_scatter(y1_part, 'a2', scatter_dimension=2, tiled=True)  91.3 us
    reduce_scatter x1, waiting for transfers between devices, local_sweep(): lax.psum_scatter(y3_part, 'a2', scatter_dimension=2, tiled=True)  77.2 us
    dot_general x1, matrix products, local_sweep(): jnp.dot(tensor.reshape(frames * grid_h, grid_w), rows_of(u_width, 'a3', g...  60.4 us
  transfers between devices with their start and end apart: 8, of which 5 were waited for; matrix products, arithmetic and copies ran while one was open for 16% of the time, Pallas kernels for 0%

commit v1 on v0

v1 whole, which is shorter than its diff:
```python
import functools

import jax
import jax.numpy as jnp
from jax import lax
from jax.experimental import pallas as pl
from jax.experimental.pallas import tpu as pltpu
from jax.sharding import PartitionSpec as P

MESH = pl.DeviceIdType.MESH
F32, BF16 = jnp.float32, jnp.bfloat16
NT = (((1,), (1,)), ((), ()))

FR, GH, GW = 192, 360, 720
RT, RH, RW = 48, 88, 176
CH = 16
NCH = FR // CH
POS = CH * GH
NSUB = 3
SUB = POS // NSUB
CW = RW // 2
HP = 384
CL = 24


def coords():
    return lax.axis_index('a3'), lax.axis_index('a2'), lax.axis_index('a1')


def peer(me, k):
    flips = (k >> 2, (k >> 1) & 1, k & 1)
    return tuple(1 - m if f else m for m, f in zip(me, flips))


def flat(dev):
    return (dev[0] * 2 + dev[1]) * 2 + dev[2]


def remote(src, dst, send_sem, recv_sem, dev):
    return pltpu.make_async_remote_copy(src_ref=src, dst_ref=dst, send_sem=send_sem, recv_sem=recv_sem, device_id=dev, device_id_type=MESH)


def greet_all(me):
    barrier = pltpu.get_barrier_semaphore()
    for k in range(1, 8):
        pl.semaphore_signal(barrier, inc=1, device_id=peer(me, k), device_id_type=MESH)
    pl.semaphore_wait(barrier, 7)


def first_column(dev):
    return dev[1] * 40 + dev[2] * CL


def duplicate_rows(dev):
    return dev[1] * (1 - dev[2]) * (8 * CH)


def time_kernel(x_hbm, u3t_ref, u2p_ref, u1_ref, t_out, u1_out, xbuf, own, send, recv, sbuf, tbuf, t3, y1b, gram, gslots, pall,
                xsem, ysend, yrecv, credit, qsend, qrecv, gsend, grecv, psend, precv, osem):
    me = coords()
    y_peer = peer(me, 4)
    greet_all(me)

    def fetch(s, k):
        start = pl.multiple_of(s * POS + k * SUB, SUB)
        return pltpu.make_async_copy(x_hbm.at[pl.ds(start, SUB), :], xbuf.at[k], xsem.at[k])

    def lanes(k):
        return pl.ds(pl.multiple_of(k * SUB, 128), SUB)

    def ycopy(slot, k):
        return remote(send.at[slot, :, lanes(k)], recv.at[slot, :, lanes(k)], ysend.at[slot, k], yrecv.at[slot, k], y_peer)

    def qcopy(slot, q, t, src_dev):
        return remote(tbuf.at[slot, q - 1], t3.at[src_dev[2], t, src_dev[1]], qsend.at[slot, q - 1], qrecv.at[q - 1, t], peer(me, q))

    for k in range(NSUB):
        fetch(0, k).start()

    def produce(s):
        slot = lax.rem(s, 2)

        @pl.when(s >= 2)
        def _():
            pl.semaphore_wait(credit, 1)
            for k in range(NSUB):
                ycopy(slot, k).wait_send()

        def sub(k, carry):
            fetch(s, k).wait()
            part = lax.dot_general(u3t_ref[...], xbuf[k], NT, preferred_element_type=F32)
            own[slot, :, lanes(k)] = part[:CW]
            send[slot, :, lanes(k)] = part[CW:]
            ycopy(slot, k).start()

            @pl.when(s < NCH - 1)
            def _():
                fetch(s + 1, k).start()

            return carry

        lax.fori_loop(0, NSUB, sub, 0)

    def combine(t):
        slot = lax.rem(t, 2)
        for k in range(NSUB):
            ycopy(slot, k).wait_recv()
        lane = lax.broadcasted_iota(jnp.int32, (CW, 128), 1)
        for ii in range(CH):
            start = (ii * GH) // 128 * 128
            off = ii * GH - start
            wid = min(512, POS - start)
            blk = own[slot, :, start:start + wid] + recv[slot, :, start:start + wid]
            if off:
                blk = pltpu.roll(blk, wid - off, 1)
            for lt in range(3):
                piece = blk[:, lt * 128:(lt + 1) * 128]
                sbuf[lt, pl.ds(ii, CW, stride=CH), :] = piece if lt < 2 else jnp.where(lane < GH - 256, piece, 0.0)

        @pl.when(t < NCH - 2)
        def _():
            pl.semaphore_signal(credit, inc=1, device_id=y_peer, device_id_type=MESH)

        @pl.when(t >= 2)
        def _():
            for q in range(1, 4):
                qcopy(slot, q, t - 2, me).wait_send()

        row = lax.broadcasted_iota(jnp.int32, (CL * CH, 128), 0)

        def part_for(dev, put):
            for lt in range(3):
                v = sbuf[lt, pl.ds(pl.multiple_of(first_column(dev) * CH, 8), CL * CH), :]
                put(slice(lt * 128, (lt + 1) * 128), jnp.where(row < duplicate_rows(dev), 0.0, v).astype(BF16))

        for q in range(1, 4):
            def put_peer(ls, v):
                tbuf[slot, q - 1, :, ls] = v

            part_for(peer(me, q), put_peer)
            qcopy(slot, q, t, me).start()

        def put_own(ls, v):
            t3[me[2], t, me[1], :, ls] = v

        part_for(me, put_own)

    def height(t):
        for q in range(1, 4):
            qcopy(0, q, t, peer(me, q)).wait_recv()
        for aa in range(2):
            acc = jnp.dot(t3[aa, t, 0], u2p_ref[0], preferred_element_type=F32)
            acc = acc + jnp.dot(t3[aa, t, 1], u2p_ref[1], preferred_element_type=F32)
            acc = acc.astype(BF16).reshape(CL // 2, 2, CH, 128)
            rows = pl.ds(pl.multiple_of(aa * FR + t * CH, CH), CH)
            y1b[:, rows, 0:128] = acc[:, 0]
            y1b[:, rows, 128:256] = acc[:, 1]

    def step(s, carry):
        @pl.when(s < NCH)
        def _():
            produce(s)

        @pl.when((s >= 1) & (s <= NCH))
        def _():
            combine(s - 1)

        @pl.when(s >= 2)
        def _():
            height(s - 2)

        return carry

    lax.fori_loop(0, NCH + 2, step, 0)

    for slot in range(2):
        for k in range(NSUB):
            ycopy(slot, k).wait_send()
        for q in range(1, 4):
            qcopy(slot, q, NCH - 2 + slot, me).wait_send()

    keep = pltpu.make_async_copy(t3, t_out, osem)
    keep.start()

    acc = lax.dot_general(y1b[0], y1b[0], NT, preferred_element_type=F32)
    for c in range(1, CL // 2):
        acc = acc + lax.dot_general(y1b[c], y1b[c], NT, preferred_element_type=F32)
    gram[...] = acc

    def rows_of(dev):
        return pl.ds(pl.multiple_of(flat(dev) * RT, 8), RT)

    def gcopy(k):
        return remote(gram.at[rows_of(peer(me, k))], gslots.at[k - 1], gsend.at[k - 1], grecv.at[k - 1], peer(me, k))

    for k in range(1, 8):
        gcopy(k).start()
    total = gram[rows_of(me), :]
    for k in range(1, 8):
        gcopy(k).wait_recv()
        total = total + gslots[k - 1]
    pall[flat(me)] = jnp.dot(total.astype(BF16), u1_ref[...], preferred_element_type=F32)

    def pcopy(k, dev):
        return remote(pall.at[flat(me)], pall.at[flat(dev)], psend.at[k - 1], precv.at[k - 1], peer(me, k))

    for k in range(1, 8):
        pcopy(k, me).start()
    for k in range(1, 8):
        pcopy(k, peer(me, k)).wait_recv()
    power = pall[...].reshape(8 * RT, 128)[:, :RT]
    u1_out[...] = power / jnp.sqrt(jnp.sum(power * power, axis=0, keepdims=True))
    for k in range(1, 8):
        gcopy(k).wait_send()
        pcopy(k, me).wait_send()
    keep.wait()


def time_phase(x2d, u3t, u2p, u1p):
    vmem, anym = pl.BlockSpec(memory_space=pltpu.VMEM), pl.BlockSpec(memory_space=pl.ANY)
    dma = pltpu.SemaphoreType.DMA
    return pl.pallas_call(
        time_kernel,
        name='time_phase',
        out_shape=(jax.ShapeDtypeStruct((2, NCH, 2, CL * CH, HP), BF16), jax.ShapeDtypeStruct((2 * FR, RT), F32)),
        in_specs=[anym, vmem, vmem, vmem],
        out_specs=(anym, vmem),
        scratch_shapes=[
            pltpu.VMEM((NSUB, SUB, GW), BF16), pltpu.VMEM((2, CW, POS), F32), pltpu.VMEM((2, CW, POS), F32), pltpu.VMEM((2, CW, POS), F32),
            pltpu.VMEM((3, CW * CH, 128), F32), pltpu.VMEM((2, 3, CL * CH, HP), BF16), pltpu.VMEM((2, NCH, 2, CL * CH, HP), BF16),
            pltpu.VMEM((CL // 2, 2 * FR, 256), BF16), pltpu.VMEM((2 * FR, 2 * FR), F32), pltpu.VMEM((7, RT, 2 * FR), F32), pltpu.VMEM((8, RT, 128), F32),
            dma((NSUB,)), dma((2, NSUB)), dma((2, NSUB)), pltpu.SemaphoreType.REGULAR, dma((2, 3)), dma((3, NCH)),
            dma((7,)), dma((7,)), dma((7,)), dma((7,)), dma(()),
        ],
        compiler_params=pltpu.CompilerParams(collective_id=0, has_side_effects=True, vmem_limit_bytes=60 << 20),
    )(x2d, u3t, u2p, u1p)


def rows_of(factor, axis_name, count):
    start_row = lax.axis_index(axis_name) * count
    return lax.dynamic_slice_in_dim(factor, start_row, count, 0).astype(BF16)


def gram_update(local_rows, row_axes, sum_axes, factor):
    all_rows = lax.all_gather(local_rows, row_axes, axis=0, tiled=True)
    gram_part = lax.dot_general(local_rows, all_rows, NT, preferred_element_type=F32)
    gram_rows = lax.psum(gram_part, sum_axes).astype(BF16)
    power_cols = jnp.dot(gram_rows, factor.astype(BF16), preferred_element_type=F32)
    col_sq = lax.psum(jnp.sum(power_cols * power_cols, axis=0, keepdims=True), row_axes)
    return lax.all_gather(power_cols / jnp.sqrt(col_sq), row_axes, axis=0, tiled=True)


def solution(mesh):
    def local_sweep(tensor, u_time, u_height, u_width):
        frames, grid_h, grid_w = tensor.shape
        y = lax.axis_index('a3')
        u3 = rows_of(u_width, 'a3', grid_w).T
        u3t = jnp.concatenate([lax.dynamic_slice_in_dim(u3, y * CW, CW, 0), lax.dynamic_slice_in_dim(u3, (1 - y) * CW, CW, 0)], 0)
        u2p = jnp.pad(u_height.astype(BF16).reshape(2, grid_h, RH), ((0, 0), (0, HP - grid_h), (0, 128 - RH)))
        u1p = jnp.pad(u_time.astype(BF16), ((0, 0), (0, 128 - RT)))
        t3, new_time = time_phase(tensor.reshape(frames * grid_h, grid_w), u3t, u2p, u1p)
        t3 = t3.reshape(2, NCH, 2, CL, CH, HP)
        y_two = jnp.einsum('Asxcih,Asir->xcrh', t3, new_time.astype(BF16).reshape(2, NCH, CH, RT), preferred_element_type=F32).astype(BF16)
        gram_part = jnp.einsum('xcrh,zcrk->xhzk', y_two, y_two, preferred_element_type=F32)[:, :grid_h, :, :grid_h].reshape(2 * grid_h, 2 * grid_h)
        gram_two = lax.psum(gram_part, ('a1', 'a2', 'a3')).astype(BF16)
        power = jnp.dot(gram_two, u_height.astype(BF16), preferred_element_type=F32)
        new_height = power / jnp.sqrt(jnp.sum(power * power, axis=0, keepdims=True))

        time_rows = rows_of(new_time, 'a1', frames)
        z_part = lax.dot_general(time_rows, tensor, (((0,), (0,)), ((), ())), preferred_element_type=F32)
        z_mat = lax.psum_scatter(z_part, 'a1', scatter_dimension=0, tiled=True).astype(BF16)
        y3_part = jnp.einsum('ahw,hb->wab', z_mat, rows_of(new_height, 'a2', grid_h), preferred_element_type=F32)
        y_three = lax.psum_scatter(y3_part, 'a2', scatter_dimension=2, tiled=True).astype(BF16)
        new_width = gram_update(y_three.reshape(grid_w, -1), 'a3', ('a1', 'a2'), u_width)
        core_part = jnp.einsum('wab,wc->abc', y_three, rows_of(new_width, 'a3', grid_w), preferred_element_type=F32)
        core_tensor = lax.psum_scatter(core_part, 'a3', scatter_dimension=2, tiled=True)
        core_energy = lax.psum(jnp.sum(core_tensor * core_tensor), ('a1', 'a2', 'a3'))
        return new_time, new_height, new_width, core_tensor, core_energy

    return jax.shard_map(local_sweep, mesh=mesh, in_specs=(P('a1', 'a2', 'a3'), P(), P(), P()), out_specs=(P(), P(), P(), P('a1', 'a2', 'a3'), P()), check_vma=False)
```

time: 2050 us -> 1140 us (0.56)
  waiting for transfers between devices: 950 us -> 152 us
  Pallas kernels: 0 us -> 562 us
  local copies, waits for them, and re-layouts: 475 us -> 29 us
  blocking collectives: 401 us -> 235 us
  matrix products: 160 us -> 123 us
    reduce_scatter x3 -> x1, waiting for transfers between devices: 796 us -> 0.02 us  [local_sweep(): lax.psum_scatter(z_part, 'a1', scatter_dimension=0, tiled=True).astype(BF16)]
    pallas_call x0 -> x1, Pallas kernels: none -> 562 us  [time_phase(): pl.pallas_call(time_kernel, name='time_phase', out_shape=(jax.ShapeDtypeS...]
    reshape x7 -> x1, local copies, waits for them, and re-layouts: 401 us -> 3.02 us  [local_sweep(): jnp.einsum('xcrh,zcrk->xhzk', y_two, y_two, preferred_element_type=F32)]
    unnamed x1 -> x0, blocking collectives: 130 us -> none
    dot_general x10 -> x6, matrix products: 151 us -> 115 us  [the longest x1 97.3 us: local_sweep(): lax.dot_general(time_rows, tensor, (((0,), (0,)), ((), ())), preferred_el...]
    convert_element_type x3, local copies, waits for them, and re-layouts: 35.6 us -> 1.5 us  [the longest x1 1.22 us: rows_of(): return lax.dynamic_slice_in_dim(factor, start_row, count, 0).astype(BF16)]
    psum x3 -> x2, blocking collectives: 215 us -> 195 us  [the longest x1 153 us: gram_update(): gram_rows = lax.psum(gram_part, sum_axes).astype(BF16)]
    all_gather x3 -> x1, waiting for transfers between devices: 41.4 us -> 41.3 us  [gram_update(): all_rows = lax.all_gather(local_rows, row_axes, axis=0, tiled=True)]
  transfers between devices with their start and end apart: 8 -> 4, of which waited for: 5 -> 3; matrix products, arithmetic and copies ran while one was open for 16% -> 2% of each run, Pallas kernels for 0% -> 0%
where the time goes in v1:
time: 1140 us; the launch traced here: 1130 us
  Pallas kernels  562 us (49%)
  blocking collectives  235 us (21%)
  waiting for transfers between devices  152 us (13%)
  matrix products  123 us (11%)
  local copies, waits for them, and re-layouts  29 us (3%)
  other arithmetic  16.4 us (1%)
  between operations  15 us (1%)
    pallas_call x1, Pallas kernels, time_phase(): pl.pallas_call(time_kernel, name='time_phase', out_shape=(jax.ShapeDtypeS...  562 us
    psum x1, blocking collectives, gram_update(): gram_rows = lax.psum(gram_part, sum_axes).astype(BF16)  153 us
    dot_general x1, matrix products, local_sweep(): lax.dot_general(time_rows, tensor, (((0,), (0,)), ((), ())), preferred_el...  97.3 us
    reduce_scatter x1, waiting for transfers between devices, local_sweep(): lax.psum_scatter(y3_part, 'a2', scatter_dimension=2, tiled=True)  76.4 us
    psum x1, blocking collectives, local_sweep(): gram_two = lax.psum(gram_part, ('a1', 'a2', 'a3')).astype(BF16)  42.2 us
    all_gather x1, waiting for transfers between devices, gram_update(): all_rows = lax.all_gather(local_rows, row_axes, axis=0, tiled=True)  41.3 us
    unnamed x5, waiting for transfers between devices  34.5 us
  transfers between devices with their start and end apart: 4, of which 3 were waited for; matrix products, arithmetic and copies ran while one was open for 2% of the time, Pallas kernels for 0%

profile of v1, /device:TPU:0, one launch (start us, length us, event | category | flops | bytes accessed | tf_op | source)
XLA Modules:
  0.0 1133.6 jit_solution(786581988339309681)
XLA Ops:
  7.2 1.0 convert_element_type.48
  8.4 0.9 convert_element_type.49
  10.8 1.2 dynamic-slice_convert_fusion.1
  12.8 562.1 %time_phase.1 = (bf16[2,12,2,384,384]{4,3,2,1,0:T(8,128)(2,1)}, f32[384,48]{1,0:T(8,128)}) custom-call(bf16[69120,720]{1,0:T(8,128)(2,1)} %bitcast.x_hbm, bf16[176,720]{1,0:T(8,128)(2,1)} %pad_maximum_fusion.u3t_ref, bf16[2,384,128]{2,1,0:T(8,128)(2,1)} %pad.8.u2p_ref, bf16[384,128]{1,0:T(8,128)(2,1)} %pad.9.u1_ref), custom_call_target="tpu_custom_call" | custom-call | tf_op jit(solution)/shard_map/time_phase/pallas_call | solution.py:222
  574.9 97.3 %fusion = f32[48,360,720]{2,0,1:T(8,128)} fusion(bf16[192,360,720]{2,1,0:T(8,128)(2,1)} %param.4, f32[384,48]{1,0:T(8,128)} %get-tuple-element.24, s32[]{:T(128)S(6)} %select_n.20), kind=kOutput, calls=%fused_computation | convolution fusion | flops 4777574400 | bytes 155983872 | tf_op jit(solution)/shard_map/dot_general | solution.py:270
  673.1 7.4 bitcast_convert_fusion
  680.6 1.8 fusion.12
  682.5 2.6 copy.38
  685.1 3.0 reshape.36
  688.1 42.2 %all-reduce.8 = bf16[720,720]{1,0:T(8,128)(2,1)S(1)} all-reduce(f32[720,720]{1,0:T(8,128)S(1)} %reshape.36), channel_id=1, replica_groups=mesh['a3'=2,'a2'=2,'a1'=2] {'a1','a2','a3'}, use_global_device_ids=true, to_apply=%region_0.1 | all-reduce | flops 518400 | bytes 3110400 | tf_op jit(solution)/shard_map/psum | solution.py:265
  731.0 9.4 convert_element_type.56
  740.4 4.7 fusion.4
  745.1 4.7 copy.42
  749.8 76.4 %reduce-scatter.6.cloned.1.call-done = f32[720,24,44]{0,1,2:T(8,128)} async-done(((f32[720,24,88]{0,1,2:T(8,128)}), f32[720,24,44]{0,1,2:T(8,128)}) %reduce-scatter.6.cloned.1.call-update) | async-done | bytes 3041296 | tf_op jit(solution)/shard_map/reduce_scatter | solution.py:273
  826.3 2.1 convert_element_type.57
  828.4 1.2 copy-done
  829.9 2.1 reshape.38
  832.1 2.1 reshape.37
  834.1 41.3 %all-gather.4.cloned.1.call-done = bf16[2,720,1056]{1,2,0:T(8,128)(2,1)} async-done(((bf16[1,720,1056]{1,2,0:T(8,128)(2,1)}), bf16[2,720,1056]{1,2,0:T(8,128)(2,1)}) %all-gather.4.cloned.1.call-update) | async-done | bytes 3041296 | tf_op jit(solution)/shard_map/all_gather | solution.py:245
  875.5 4.3 copy.45
  879.7 6.2 fusion.31
  886.0 152.6 %all-reduce.9 = bf16[720,1440]{1,0:T(8,128)(2,1)S(1)} all-reduce(f32[720,1440]{1,0:T(8,128)} %fusion.31), channel_id=1, replica_groups=mesh['a3'=2,'a2'=2,'a1'=2] {'a1','a2'}, use_global_device_ids=true, to_apply=%region_4.5 | all-reduce | flops 1036800 | bytes 6220800 | tf_op jit(solution)/shard_map/psum | solution.py:247
  1038.6 2.2 multiply_reduce_fusion.1
  1040.7 4.9 psum.30
  1045.8 13.2 %all-gather.1 = f32[2,720,176]{1,2,0:T(8,128)S(1)} all-gather(f32[1,720,176]{1,2,0:T(8,128)S(1)} %divide_bitcast_fusion), channel_id=1, replica_groups=mesh['a3'=2,'a2'=2,'a1'=2] {'a3'}, dimensions={0}, use_global_device_ids=true | all-gather | bytes 1520640 | tf_op jit(solution)/shard_map/all_gather | solution.py:250
  1059.0 0.8 copy.46
  1059.9 1.9 reshape.41
  1061.8 2.9 fusion.21
  1066.7 34.4 %all-reduce.7.cloned.1.call-done = f32[24,44,176]{2,1,0:T(8,128)} async-done(((f32[24,44,176]{2,1,0:T(8,128)}), f32[24,44,176]{2,1,0:T(8,128)}) %all-reduce.7.cloned.1.call-update) | async-done | bytes 743440
  1101.1 2.1 multiply_reduce_fusion
  1103.2 1.0 copy.49
  1104.2 22.4 %psum.31 = f32[]{:T(128)} all-reduce(f32[]{:T(128)} %get-tuple-element.29), channel_id=1, replica_groups=mesh['a3'=2,'a2'=2,'a1'=2] {'a1','a2','a3'}, use_global_device_ids=true, to_apply=%region_9.10 | all-reduce | flops 1 | bytes 8 | tf_op jit(solution)/shard_map/psum | solution.py:277
  (36 shorter events, 6.2 us)
Async XLA Ops:
  7.2 723.8 %reduce-scatter.4.cloned.1.call-start = ((), (), s32[]{:S(2)}) async-start(), calls=%async_computation.2 | async-start | bytes 79626240 | tf_op jit(solution)/shard_map/reduce_scatter | solution.py:271
  672.2 0.9 copy-start.2
  672.2 154.1 %reduce-scatter.6.cloned.1.call-start = ((), (), s32[]{:S(2)}) async-start(), calls=%async_computation.3 | async-start | bytes 9732096 | tf_op jit(solution)/shard_map/reduce_scatter | solution.py:273
  730.9 9.4 copy-start.4
  749.8 125.7 %all-gather.4.cloned.1.call-start = ((), (), s32[]{:S(2)}) async-start(), calls=%async_computation.4 | async-start | bytes 4866048 | tf_op jit(solution)/shard_map/all_gather | solution.py:245
  828.4 1.2 copy-start
  832.0 269.1 %all-reduce.7.cloned.1.call-start = ((), (), s32[]{:S(2)}) async-start(), calls=%async_computation.5 | async-start | bytes 2359296
  1059.0 2.8 copy-start.1
  1061.8 2.9 copy-start.3
  1061.8 3.7 copy-start.5
Sparse Core Ops, SparseCore 0:
  672.3 51.6 reduce-scatter.3
  749.9 76.3 reduce-scatter.5
  832.1 43.2 all-gather.3
  1064.8 36.2 all-reduce.6

commit v2 on v1

--- a/solution.py
+++ b/solution.py
@@ -236,18 +236,183 @@
     )(x2d, u3t, u2p, u1p)
 
 
+NPAIR = 12
+PR = RH
+WP = 768
+WQ = WP // 4
+
+
+def width_kernel(z_hbm, u2t_ref, u3p_ref, u3_out, g_out, e_out, zbuf, own, send, recv, y3, acc, core_in, x_in, pall, u3b, energy,
+                 zsem, xsend, xrecv, ysend, yrecv, csend, crecv, rsend, rrecv, psend, precv, fsend, frecv, esend, erecv):
+    me = coords()
+    y, x, a = me
+    x_peer, y_peer, c_peer = peer(me, 2), peer(me, 4), peer(me, 1)
+    greet_all(me)
+
+    def fetch(p, slot):
+        return pltpu.make_async_copy(z_hbm.at[pl.ds(p * 2, 2)], zbuf.at[slot], zsem.at[slot])
+
+    def xcopy(p):
+        return remote(send.at[p], recv.at[p], xsend.at[p], xrecv.at[p], x_peer)
+
+    def ycopy(p):
+        return remote(y3.at[0, p], y3.at[1, p], ysend.at[p], yrecv.at[p], y_peer)
+
+    fetch(0, 0).start()
+    acc[...] = jnp.zeros_like(acc)
+
+    def produce(p, carry):
+        slot = lax.rem(p, 2)
+        fetch(p, slot).wait()
+
+        @pl.when(p < NPAIR - 1)
+        def _():
+            fetch(p + 1, 1 - slot).start()
+
+        for r in range(2):
+            part = jnp.dot(u2t_ref[...], zbuf[slot, r], preferred_element_type=F32)
+            own[p, r * 44:(r + 1) * 44] = part[0:44]
+            send[p, r * 44:(r + 1) * 44] = part[48:92]
+        xcopy(p).start()
+        return carry
+
+    lax.fori_loop(0, NPAIR, produce, 0)
+
+    def add_gram(p):
+        ycopy(p).wait_recv()
+
+        def block(m, carry):
+            cols = pl.ds(pl.multiple_of(m * 128, 128), 128)
+            lhs = y3[0, p, :, cols]
+            for half in range(2):
+                add = lax.dot_general(lhs, y3[half, p], (((0,), (0,)), ((), ())), preferred_element_type=F32)
+                acc[cols, half * WP:(half + 1) * WP] += add
+            return carry
+
+        lax.fori_loop(0, WP // 128, block, 0)
+
+    def consume(p, carry):
+        @pl.when(p < NPAIR)
+        def _():
+            xcopy(p).wait_recv()
+            y3[0, p, :, 640:768] = jnp.zeros((PR, 128), BF16)
+            y3[0, p, :, 0:GW] = (own[p] + recv[p]).astype(BF16)
+            ycopy(p).start()
+
+        @pl.when(p >= 1)
+        def _():
+            add_gram(p - 1)
+
+        return carry
+
+    lax.fori_loop(0, NPAIR + 1, consume, 0)
+
+    def quarter(core, side):
+        return pl.ds(pl.multiple_of(core * 2 * WQ + side * WQ, 8), WQ)
+
+    def ccopy(i):
+        side = 1 - x if i == 0 else x
+        return remote(acc.at[quarter(1 - a, side)], core_in.at[i], csend.at[i], crecv.at[i], c_peer)
+
+    ccopy(0).start()
+    ccopy(1).start()
+    ccopy(0).wait_recv()
+    acc[quarter(a, 1 - x), :] += core_in[0]
+    rcopy = remote(acc.at[quarter(a, 1 - x)], x_in, rsend, rrecv, x_peer)
+    rcopy.start()
+    ccopy(1).wait_recv()
+    rows = acc[quarter(a, x), :] + core_in[1]
+    rcopy.wait_recv()
+    rows = (rows + x_in[...]).astype(BF16)
+
+    def slot_of(dev):
+        return dev[0] * 4 + dev[2] * 2 + dev[1]
+
+    mine = slot_of(me)
+    pall[mine] = jnp.dot(rows, u3p_ref[...], preferred_element_type=F32)
+
+    def pcopy(i, dev):
+        return remote(pall.at[slot_of(dev)], pall.at[slot_of(dev)], psend.at[i], precv.at[i], peer(me, (2, 4, 6)[i]))
+
+    def fcopy(i, dev):
+        return remote(pall.at[slot_of(dev)], pall.at[slot_of(dev)], fsend.at[i], frecv.at[i], c_peer)
+
+    for i in range(3):
+        pcopy(i, me).start()
+    fcopy(3, me).start()
+    for i in range(3):
+        dev = peer(me, (2, 4, 6)[i])
+        pcopy(i, dev).wait_recv()
+        fcopy(i, dev).start()
+    for i in range(3):
+        fcopy(i, peer(c_peer, (2, 4, 6)[i])).wait_recv()
+    fcopy(3, c_peer).wait_recv()
+    power = pall[...].reshape(2 * WP, 256)
+    lane = lax.broadcasted_iota(jnp.int32, (1, 256), 1)
+    norm = jnp.where(lane < RW, jnp.sqrt(jnp.sum(power * power, axis=0, keepdims=True)), 1.0)
+    fresh = power / norm
+    u3_out[0:GW, :] = fresh[0:GW, :RW]
+    u3_out[GW:2 * GW, :] = fresh[WP:WP + GW, :RW]
+    half = pltpu.roll(fresh, 256 - y * CW, 1)[:, :128].astype(BF16)
+    u3b[...] = half.reshape(2, WP, 128)
+
+    def core_rows(p, esum):
+        g = jnp.dot(y3[0, p], u3b[y], preferred_element_type=F32) + jnp.dot(y3[1, p], u3b[1 - y], preferred_element_type=F32)
+        g = jnp.where(lane[:, :128] < CW, g, 0.0)
+        g_out[p] = g[:, :CW]
+        return esum + jnp.sum((g * g).reshape(PR // 8, 8, 128), axis=0)
+
+    energy[flat(me)] = lax.fori_loop(0, NPAIR, core_rows, jnp.zeros((8, 128), F32))
+
+    def ecopy(k, dev):
+        return remote(energy.at[flat(dev)], energy.at[flat(dev)], esend.at[k - 1], erecv.at[k - 1], peer(me, k))
+
+    for k in range(1, 8):
+        ecopy(k, me).start()
+    for k in range(1, 8):
+        ecopy(k, peer(me, k)).wait_recv()
+    e_out[...] = jnp.sum(jnp.sum(energy[...], axis=0), axis=(0, 1), keepdims=True)
+
+    def drain(p, carry):
+        xcopy(p).wait_send()
+        ycopy(p).wait_send()
+        return carry
+
+    lax.fori_loop(0, NPAIR, drain, 0)
+    ccopy(0).wait_send()
+    ccopy(1).wait_send()
+    rcopy.wait_send()
+    for i in range(3):
+        pcopy(i, me).wait_send()
+    for i in range(4):
+        fcopy(i, me).wait_send()
+    for k in range(1, 8):
+        ecopy(k, me).wait_send()
+
+
+def width_phase(z_mat, u2t, u3p):
+    vmem, anym = pl.BlockSpec(memory_space=pltpu.VMEM), pl.BlockSpec(memory_space=pl.ANY)
+    dma = pltpu.SemaphoreType.DMA
+    return pl.pallas_call(
+        width_kernel,
+        name='width_phase',
+        out_shape=(jax.ShapeDtypeStruct((2 * GW, RW), F32), jax.ShapeDtypeStruct((NPAIR, PR, CW), F32), jax.ShapeDtypeStruct((1, 1), F32)),
+        in_specs=[anym, vmem, vmem],
+        out_specs=(vmem, vmem, vmem),
+        scratch_shapes=[
+            pltpu.VMEM((2, 2, GH, GW), BF16), pltpu.VMEM((NPAIR, PR, GW), F32), pltpu.VMEM((NPAIR, PR, GW), F32), pltpu.VMEM((NPAIR, PR, GW), F32),
+            pltpu.VMEM((2, NPAIR, PR, WP), BF16), pltpu.VMEM((WP, 2 * WP), F32), pltpu.VMEM((2, WQ, 2 * WP), F32), pltpu.VMEM((WQ, 2 * WP), F32),
+            pltpu.VMEM((8, WQ, 256), F32), pltpu.VMEM((2, WP, 128), BF16), pltpu.VMEM((8, 8, 128), F32),
+            dma((2,)), dma((NPAIR,)), dma((NPAIR,)), dma((NPAIR,)), dma((NPAIR,)), dma((2,)), dma((2,)), dma(()), dma(()),
+            dma((3,)), dma((3,)), dma((4,)), dma((4,)), dma((7,)), dma((7,)),
+        ],
+        compiler_params=pltpu.CompilerParams(collective_id=1, has_side_effects=True, vmem_limit_bytes=60 << 20),
+    )(z_mat, u2t, u3p)
+
+
 def rows_of(factor, axis_name, count):
     start_row = lax.axis_index(axis_name) * count
     return lax.dynamic_slice_in_dim(factor, start_row, count, 0).astype(BF16)
-
-
-def gram_update(local_rows, row_axes, sum_axes, factor):
-    all_rows = lax.all_gather(local_rows, row_axes, axis=0, tiled=True)
-    gram_part = lax.dot_general(local_rows, all_rows, NT, preferred_element_type=F32)
-    gram_rows = lax.psum(gram_part, sum_axes).astype(BF16)
-    power_cols = jnp.dot(gram_rows, factor.astype(BF16), preferred_element_type=F32)
-    col_sq = lax.psum(jnp.sum(power_cols * power_cols, axis=0, keepdims=True), row_axes)
-    return lax.all_gather(power_cols / jnp.sqrt(col_sq), row_axes, axis=0, tiled=True)
 
 
 def solution(mesh):
@@ -269,12 +434,15 @@
         time_rows = rows_of(new_time, 'a1', frames)
         z_part = lax.dot_general(time_rows, tensor, (((0,), (0,)), ((), ())), preferred_element_type=F32)
         z_mat = lax.psum_scatter(z_part, 'a1', scatter_dimension=0, tiled=True).astype(BF16)
-        y3_part = jnp.einsum('ahw,hb->wab', z_mat, rows_of(new_height, 'a2', grid_h), preferred_element_type=F32)
-        y_three = lax.psum_scatter(y3_part, 'a2', scatter_dimension=2, tiled=True).astype(BF16)
-        new_width = gram_update(y_three.reshape(grid_w, -1), 'a3', ('a1', 'a2'), u_width)
-        core_part = jnp.einsum('wab,wc->abc', y_three, rows_of(new_width, 'a3', grid_w), preferred_element_type=F32)
-        core_tensor = lax.psum_scatter(core_part, 'a3', scatter_dimension=2, tiled=True)
-        core_energy = lax.psum(jnp.sum(core_tensor * core_tensor), ('a1', 'a2', 'a3'))
+        x = lax.axis_index('a2')
+        u2r = rows_of(new_height, 'a2', grid_h).T
+        own_b, other_b = lax.dynamic_slice_in_dim(u2r, x * 44, 44, 0), lax.dynamic_slice_in_dim(u2r, (1 - x) * 44, 44, 0)
+        u2t = jnp.concatenate([jnp.pad(own_b, ((0, 4), (0, 0))), jnp.pad(other_b, ((0, 4), (0, 0)))], 0)
+        u3y = jnp.pad(u_width.astype(BF16).reshape(2, grid_w, RW), ((0, 0), (0, WP - grid_w), (0, 256 - RW)))
+        u3p = jnp.concatenate([lax.dynamic_slice_in_dim(u3y, y, 1, 0), lax.dynamic_slice_in_dim(u3y, 1 - y, 1, 0)], 0).reshape(2 * WP, 256)
+        new_width, core_tensor, core_energy = width_phase(z_mat, u2t, u3p)
+        core_tensor = core_tensor.reshape(RT // 2, RH // 2, CW)
+        core_energy = core_energy.reshape(())
         return new_time, new_height, new_width, core_tensor, core_energy
 
     return jax.shard_map(local_sweep, mesh=mesh, in_specs=(P('a1', 'a2', 'a3'), P(), P(), P()), out_specs=(P(), P(), P(), P('a1', 'a2', 'a3'), P()), check_vma=False)

time: 1140 us -> 931 us (0.82)
  blocking collectives: 235 us -> 42.2 us
  waiting for transfers between devices: 152 us -> 0.02 us
  Pallas kernels: 562 us -> 694 us
  local copies, waits for them, and re-layouts: 29 us -> 51.8 us
  matrix products: 123 us -> 107 us
    psum x3 -> x0, blocking collectives: 180 us -> none  [the longest x1 153 us: gram_update(): gram_rows = lax.psum(gram_part, sum_axes).astype(BF16)]
    pallas_call x0 -> x1, Pallas kernels: none -> 132 us  [width_phase(): pl.pallas_call(width_kernel, name='width_phase', out_shape=(jax.ShapeDtyp...]
    reduce_scatter x1 -> x0, waiting for transfers between devices: 76.4 us -> none  [local_sweep(): lax.psum_scatter(y3_part, 'a2', scatter_dimension=2, tiled=True)]
    all_gather x1 -> x0, waiting for transfers between devices: 41.3 us -> none  [gram_update(): all_rows = lax.all_gather(local_rows, row_axes, axis=0, tiled=True)]
    dot_general x0 -> x1, local copies, waits for them, and re-layouts: none -> 36.1 us  [local_sweep(): lax.dot_general(time_rows, tensor, (((0,), (0,)), ((), ())), preferred_el...]
    unnamed x5 -> x1, waiting for transfers between devices: 34.5 us -> 0.02 us
    dot_general x4 -> x0, matrix products: 16 us -> none  [the longest x1 6.22 us: gram_update(): lax.dot_general(local_rows, all_rows, NT, preferred_element_type=F32)]
    all_gather x1 -> x0, blocking collectives: 13.2 us -> none  [gram_update(): lax.all_gather(power_cols / jnp.sqrt(col_sq), row_axes, axis=0, tiled=True)]
  transfers between devices with their start and end apart: 4 -> 1, of which waited for: 3 -> 0; matrix products, arithmetic and copies ran while one was open for 2% -> 2% of each run, Pallas kernels for 0% -> 0%
where the time goes in v2:
time: 931 us; the launch traced here: 930 us
  Pallas kernels  694 us (75%)
  matrix products  107 us (11%)
  local copies, waits for them, and re-layouts  51.8 us (6%)
  blocking collectives  42.2 us (5%)
  other arithmetic  18.8 us (2%)
  between operations  16 us (2%)
    pallas_call x1, Pallas kernels, time_phase(): pl.pallas_call(time_kernel, name='time_phase', out_shape=(jax.ShapeDtypeS...  562 us
    pallas_call x1, Pallas kernels, width_phase(): pl.pallas_call(width_kernel, name='width_phase', out_shape=(jax.ShapeDtyp...  132 us
    dot_general x1, matrix products, local_sweep(): lax.dot_general(time_rows, tensor, (((0,), (0,)), ((), ())), preferred_el...  97.4 us
    psum x1, blocking collectives, local_sweep(): gram_two = lax.psum(gram_part, ('a1', 'a2', 'a3')).astype(BF16)  42.2 us
    dot_general x1, local copies, waits for them, and re-layouts, local_sweep(): lax.dot_general(time_rows, tensor, (((0,), (0,)), ((), ())), preferred_el...  36.1 us
  transfers between devices with their start and end apart: 1, of which 0 were waited for; matrix products, arithmetic and copies ran while one was open for 2% of the time, Pallas kernels for 0%

profile of v2, /device:TPU:0, one launch (start us, length us, event | category | flops | bytes accessed | tf_op | source)
XLA Modules:
  0.0 930.1 jit_solution(16391957560060265879)
XLA Ops:
  7.2 0.0 reduce-scatter.2.cloned.1.call-start
  7.2 1.0 convert_element_type.44
  8.2 0.2 copy.28
  8.4 0.9 convert_element_type.45
  9.3 0.1 copy.29
  9.4 0.7 pad.19.u2p_ref
  10.1 0.7 pad.20.u1_ref
  10.8 1.2 dynamic-slice_convert_fusion
  12.1 0.7 pad_maximum_fusion.1.u3t_ref
  12.8 562.1 %time_phase.1 = (bf16[2,12,2,384,384]{4,3,2,1,0:T(8,128)(2,1)}, f32[384,48]{1,0:T(8,128)}) custom-call(bf16[69120,720]{1,0:T(8,128)(2,1)} %bitcast.x_hbm, bf16[176,720]{1,0:T(8,128)(2,1)} %pad_maximum_fusion.1.u3t_ref, bf16[2,384,128]{2,1,0:T(8,128)(2,1)} %pad.19.u2p_ref, bf16[384,128]{1,0:T(8,128)(2,1)} %pad.20.u1_ref), custom_call_target="tpu_custom_call" | custom-call | tf_op jit(solution)/shard_map/time_phase/pallas_call | solution.py:222
  574.9 97.4 %fusion = f32[48,360,720]{2,0,1:T(8,128)} fusion(bf16[192,360,720]{2,1,0:T(8,128)(2,1)} %param.4, f32[384,48]{1,0:T(8,128)} %get-tuple-element.25, s32[]{:T(128)S(6)} %select_n.30), kind=kOutput, calls=%fused_computation | convolution fusion | flops 4777574400 | bytes 155983872 | tf_op jit(solution)/shard_map/dot_general | solution.py:435
  672.3 36.1 %copy.34 = f32[48,360,720]{2,1,0:T(8,128)} copy(f32[48,360,720]{2,0,1:T(8,128)} %fusion) | data formatting | bytes 99532800 | tf_op jit(solution)/shard_map/dot_general | solution.py:435
  708.4 0.9 copy-done.3
  709.3 0.7 copy.36
  710.1 0.9 convert_element_type.53
  710.9 7.4 bitcast_convert_fusion
  718.4 1.8 fusion.5
  720.2 0.1 slice.4
  720.3 2.5 copy.31
  722.9 3.0 reshape.45
  725.9 42.2 %all-reduce.6 = bf16[720,720]{1,0:T(8,128)(2,1)S(1)} all-reduce(f32[720,720]{1,0:T(8,128)S(1)} %reshape.45), channel_id=1, replica_groups=mesh['a3'=2,'a2'=2,'a1'=2] {'a1','a2','a3'}, use_global_device_ids=true, to_apply=%region_0.1 | all-reduce | flops 518400 | bytes 3110400 | tf_op jit(solution)/shard_map/psum | solution.py:430
  768.1 0.6 multiply_reduce_fusion
  768.7 1.3 copy.45
  770.0 0.1 broadcast_divide_fusion
  770.1 0.1 dynamic-slice_convert_fusion.1
  770.3 0.6 fusion.14.u2t_ref
  770.9 0.1 pad_dynamic-slice_fusion.1
  771.1 0.9 pad_maximum_fusion
  772.0 13.7 %convert_element_type.51.z_hbm = bf16[24,360,720]{2,1,0:T(8,128)(2,1)} convert(f32[24,360,720]{2,1,0:T(8,128)} %reduce-scatter.2.cloned.1.call-done) | non-fusion elementwise | flops 6220800 | bytes 37324800 | tf_op jit(solution)/shard_map/convert_element_type | solution.py:436
  785.7 132.0 %width_phase.1 = (f32[1440,176]{1,0:T(8,128)}, f32[12,88,88]{2,1,0:T(8,128)}, f32[1,1]{1,0:T(1,128)}) custom-call(bf16[24,360,720]{2,1,0:T(8,128)(2,1)} %convert_element_type.51.z_hbm, bf16[96,360]{1,0:T(8,128)(2,1)} %fusion.14.u2t_ref, bf16[1536,256]{1,0:T(8,128)(2,1)} %bitcast.53), custom_call_target="tpu_custom_call" | custom-call | tf_op jit(solution)/shard_map/width_phase/pallas_call | solution.py:396
  917.7 2.9 copy.37
  920.6 1.0 copy.38
  (18 shorter events, 0.2 us)
Async XLA Ops:
  7.2 764.8 %reduce-scatter.2.cloned.1.call-start = ((), (), s32[]{:S(2)}) async-start(), calls=%async_computation.1 | async-start | bytes 79626240 | tf_op jit(solution)/shard_map/reduce_scatter | solution.py:436
  8.2 566.7 %copy-start.1 = (bf16[720,88]{0,1:T(8,128)(2,1)}, bf16[720,88]{0,1:T(8,128)(2,1)S(1)}, u32[]{:S(2)}) copy-start(bf16[720,88]{0,1:T(8,128)(2,1)S(1)} %convert_element_type.44) | copy-start | bytes 380164
  708.4 0.9 copy-start.3
  708.4 1.7 copy-start
  725.9 42.2 %copy-start.2 = (bf16[720,88]{0,1:T(8,128)(2,1)S(1)}, bf16[720,88]{0,1:T(8,128)(2,1)}, u32[]{:S(2)}) copy-start(bf16[720,88]{0,1:T(8,128)(2,1)} %copy-done.1) | copy-start | bytes 380164
  770.1 15.5 %copy-start.5 = (f32[720,88]{0,1:T(8,128)}, f32[720,88]{0,1:T(8,128)S(1)}, u32[]{:S(2)}) copy-start(f32[720,88]{0,1:T(8,128)S(1)} %broadcast_divide_fusion) | copy-start | bytes 760324
  917.7 2.9 copy-start.4
Sparse Core Ops, SparseCore 0:
  708.5 51.6 reduce-scatter.1

commit v3 on v2

--- a/solution.py
+++ b/solution.py
@@ -236,6 +236,187 @@
     )(x2d, u3t, u2p, u1p)
 
 
+HB = 8
+NHB = GH // HB
+GQ = 96
+TN = (((0,), (0,)), ((), ()))
+TG = 4
+AT_CHIP, AT_POWER = 4, 22
+
+
+def height_kernel(t_hbm, x_hbm, u1t_ref, u1z_ref, u2p_ref, u2_out, z_out, t3, y2, gram, core_in, chip_in, pall, kron, xbuf, zown, zsend, zrecv, zb,
+                  tsem, csend, crecv, gsend, grecv, psend, precv, xsem, dsend, drecv, credit, osem):
+    me = coords()
+    y, x, a = me
+    c_peer = peer(me, 1)
+    chips = (2, 4, 6)
+    greet_all(me)
+    width = CL * CH // TG
+
+    def tcopy(g):
+        rows = pl.ds(g * width, width)
+        return pltpu.make_async_copy(t_hbm.at[:, :, :, rows, :], t3.at[:, :, :, rows, :], tsem.at[g])
+
+    def fetch(b):
+        slot = lax.rem(b, 3)
+        return pltpu.make_async_copy(x_hbm.at[:, pl.ds(pl.multiple_of(b * HB, HB), HB), :], xbuf.at[slot], xsem.at[slot])
+
+    for g in range(TG):
+        tcopy(g).start()
+    fetch(0).start()
+    fetch(1).start()
+
+    def one_hot(shape, dim, step):
+        return (lax.broadcasted_iota(jnp.int32, shape, dim) // step == lax.broadcasted_iota(jnp.int32, shape, 1 - dim)).astype(BF16)
+
+    rep = jnp.dot(one_hot((RT * HB, RT), 0, HB), u1z_ref[...], preferred_element_type=F32).astype(BF16)
+    for i in range(0, FR * HB, 512):
+        cols = lax.broadcasted_iota(jnp.int32, (FR, 512), 1) + i
+        spread = (cols // HB == lax.broadcasted_iota(jnp.int32, (FR, 512), 0)).astype(BF16)
+        wide = jnp.dot(rep, spread, preferred_element_type=F32)
+        row = lax.broadcasted_iota(jnp.int32, (RT * HB, 512), 0)
+        col = lax.broadcasted_iota(jnp.int32, (RT * HB, 512), 1)
+        kron[:, i:i + 512] = jnp.where(lax.rem(row, HB) == lax.rem(col, HB), wide, 0.0).astype(BF16)
+
+    for g in range(TG):
+        tcopy(g).wait()
+
+        def column(c, carry):
+            for xh in range(2):
+                frames = t3[:, :, xh, pl.ds(pl.multiple_of(c * CH, CH), CH), :].reshape(2 * FR, HP)
+                y2[c, :, xh * HP:(xh + 1) * HP] = jnp.dot(u1t_ref[...], frames, preferred_element_type=F32).astype(BF16)
+            return carry
+
+        lax.fori_loop(g * (CL // TG), (g + 1) * (CL // TG), column, 0)
+
+    def gram_block(m, carry):
+        cols = pl.ds(pl.multiple_of(m * 128, 128), 128)
+        lhs = y2[:, :, cols].reshape(CL * RT, 128)
+        gram[cols, :] = lax.dot_general(lhs, y2[...].reshape(CL * RT, 2 * HP), TN, preferred_element_type=F32)
+        return carry
+
+    lax.fori_loop(0, 2 * HP // 128, gram_block, 0)
+
+    def half_of(core):
+        return pl.ds(pl.multiple_of(core * HP, HP), HP)
+
+    def rows_of(dev):
+        return pl.ds(pl.multiple_of(a * HP + (dev[1] * 2 + dev[0]) * GQ, 8), GQ)
+
+    def slot_of(dev):
+        return dev[2] * 4 + dev[1] * 2 + dev[0]
+
+    ccopy = remote(gram.at[half_of(1 - a)], core_in, csend, crecv, c_peer)
+
+    def gcopy(i):
+        dev = peer(me, chips[i])
+        return remote(gram.at[rows_of(dev)], chip_in.at[i], gsend.at[i], grecv.at[i], dev)
+
+    def pcopy(k, dev):
+        return remote(pall.at[slot_of(dev)], pall.at[slot_of(dev)], psend.at[k - 1], precv.at[k - 1], peer(me, k))
+
+    ccopy.start()
+
+    def zcopy(slot):
+        return remote(zsend.at[slot], zrecv.at[slot], dsend.at[slot], drecv.at[slot], c_peer)
+
+    def zput(b):
+        slot = lax.rem(b, 2)
+        return pltpu.make_async_copy(zb.at[slot], z_out.at[:, pl.ds(pl.multiple_of(b * HB, HB), HB), :], osem.at[slot])
+
+    def zblock(b, carry):
+        @pl.when(b < NHB)
+        def _():
+            slot = lax.rem(b, 3)
+            fetch(b).wait()
+
+            @pl.when(b < NHB - 2)
+            def _():
+                fetch(b + 2).start()
+
+            @pl.when(b >= 3)
+            def _():
+                pl.semaphore_wait(credit, 1)
+                zcopy(slot).wait_send()
+
+            part = jnp.dot(kron[...], xbuf[slot].reshape(FR * HB, GW), preferred_element_type=F32)
+            zown[slot] = part[:FR]
+            zsend[slot] = part[FR:]
+            zcopy(slot).start()
+
+        @pl.when(b >= 1)
+        def _():
+            slot = lax.rem(b - 1, 3)
+            zcopy(slot).wait_recv()
+
+            @pl.when(b >= 3)
+            def _():
+                zput(b - 3).wait()
+
+            zb[lax.rem(b - 1, 2)] = (zown[slot] + zrecv[slot]).astype(BF16).reshape(RT // 2, HB, GW)
+            zput(b - 1).start()
+
+            @pl.when(b - 1 < NHB - 3)
+            def _():
+                pl.semaphore_signal(credit, inc=1, device_id=c_peer, device_id_type=MESH)
+
+        @pl.when(b == AT_CHIP)
+        def _():
+            ccopy.wait_recv()
+            gram[half_of(a), :] += core_in[...]
+            for i in range(3):
+                gcopy(i).start()
+
+        @pl.when(b == AT_POWER)
+        def _():
+            total = gram[rows_of(me), :]
+            for i in range(3):
+                gcopy(i).wait_recv()
+                total = total + chip_in[i]
+            pall[slot_of(me)] = jnp.dot(total.astype(BF16), u2p_ref[...], preferred_element_type=F32)
+            for k in range(1, 8):
+                pcopy(k, me).start()
+
+        return carry
+
+    lax.fori_loop(0, NHB + 1, zblock, 0)
+
+    for k in range(1, 8):
+        pcopy(k, peer(me, k)).wait_recv()
+    power = pall[...].reshape(2 * HP, 128)[:, :RH]
+    fresh = power / jnp.sqrt(jnp.sum(power * power, axis=0, keepdims=True))
+    u2_out[0:GH, :] = fresh[0:GH]
+    u2_out[GH:2 * GH, :] = fresh[HP:HP + GH]
+
+    ccopy.wait_send()
+    for i in range(3):
+        gcopy(i).wait_send()
+        zcopy(i).wait_send()
+    for k in range(1, 8):
+        pcopy(k, me).wait_send()
+    zput(NHB - 2).wait()
+    zput(NHB - 1).wait()
+
+
+def height_phase(t3, tensor, u1t, u1z, u2p):
+    vmem, anym = pl.BlockSpec(memory_space=pltpu.VMEM), pl.BlockSpec(memory_space=pl.ANY)
+    dma = pltpu.SemaphoreType.DMA
+    return pl.pallas_call(
+        height_kernel,
+        name='height_phase',
+        out_shape=(jax.ShapeDtypeStruct((2 * GH, RH), F32), jax.ShapeDtypeStruct((RT // 2, GH, GW), BF16)),
+        in_specs=[anym, anym, vmem, vmem, vmem],
+        out_specs=(vmem, anym),
+        scratch_shapes=[
+            pltpu.VMEM((2, NCH, 2, CL * CH, HP), BF16), pltpu.VMEM((CL, RT, 2 * HP), BF16), pltpu.VMEM((2 * HP, 2 * HP), F32), pltpu.VMEM((HP, 2 * HP), F32),
+            pltpu.VMEM((3, GQ, 2 * HP), F32), pltpu.VMEM((8, GQ, 128), F32), pltpu.VMEM((RT * HB, FR * HB), BF16), pltpu.VMEM((3, FR, HB, GW), BF16),
+            pltpu.VMEM((3, FR, GW), F32), pltpu.VMEM((3, FR, GW), F32), pltpu.VMEM((3, FR, GW), F32), pltpu.VMEM((2, RT // 2, HB, GW), BF16),
+            dma((TG,)), dma(()), dma(()), dma((3,)), dma((3,)), dma((7,)), dma((7,)), dma((3,)), dma((3,)), dma((3,)), pltpu.SemaphoreType.REGULAR, dma((2,)),
+        ],
+        compiler_params=pltpu.CompilerParams(collective_id=2, has_side_effects=True, vmem_limit_bytes=60 << 20),
+    )(t3, tensor, u1t, u1z, u2p)
+
+
 NPAIR = 12
 PR = RH
 WP = 768
@@ -424,16 +605,12 @@
         u2p = jnp.pad(u_height.astype(BF16).reshape(2, grid_h, RH), ((0, 0), (0, HP - grid_h), (0, 128 - RH)))
         u1p = jnp.pad(u_time.astype(BF16), ((0, 0), (0, 128 - RT)))
         t3, new_time = time_phase(tensor.reshape(frames * grid_h, grid_w), u3t, u2p, u1p)
-        t3 = t3.reshape(2, NCH, 2, CL, CH, HP)
-        y_two = jnp.einsum('Asxcih,Asir->xcrh', t3, new_time.astype(BF16).reshape(2, NCH, CH, RT), preferred_element_type=F32).astype(BF16)
-        gram_part = jnp.einsum('xcrh,zcrk->xhzk', y_two, y_two, preferred_element_type=F32)[:, :grid_h, :, :grid_h].reshape(2 * grid_h, 2 * grid_h)
-        gram_two = lax.psum(gram_part, ('a1', 'a2', 'a3')).astype(BF16)
-        power = jnp.dot(gram_two, u_height.astype(BF16), preferred_element_type=F32)
-        new_height = power / jnp.sqrt(jnp.sum(power * power, axis=0, keepdims=True))
-
-        time_rows = rows_of(new_time, 'a1', frames)
-        z_part = lax.dot_general(time_rows, tensor, (((0,), (0,)), ((), ())), preferred_element_type=F32)
-        z_mat = lax.psum_scatter(z_part, 'a1', scatter_dimension=0, tiled=True).astype(BF16)
+        u1t = new_time.astype(BF16).T
+        a = lax.axis_index('a1')
+        local = lax.dynamic_slice_in_dim(u1t, a * frames, frames, 1)
+        half = RT // 2
+        u1z = jnp.concatenate([lax.dynamic_slice_in_dim(local, a * half, half, 0), lax.dynamic_slice_in_dim(local, (1 - a) * half, half, 0)], 0)
+        new_height, z_mat = height_phase(t3, tensor, u1t, u1z, u2p.reshape(2 * HP, 128))
         x = lax.axis_index('a2')
         u2r = rows_of(new_height, 'a2', grid_h).T
         own_b, other_b = lax.dynamic_slice_in_dim(u2r, x * 44, 44, 0), lax.dynamic_slice_in_dim(u2r, (1 - x) * 44, 44, 0)

time: 931 us -> 793 us (0.85)
  matrix products: 107 us -> 0 us
  Pallas kernels: 694 us -> 776 us
  local copies, waits for them, and re-layouts: 51.8 us -> 9.49 us
  blocking collectives: 42.2 us -> 0 us
  other arithmetic: 18.8 us -> 3.65 us
  between operations: 16 us -> 2.63 us
    dot_general x4 -> x0, matrix products: 107 us -> none  [the longest x1 97.4 us: local_sweep(): lax.dot_general(time_rows, tensor, (((0,), (0,)), ((), ())), preferred_el...]
    pallas_call x0 -> x1, Pallas kernels: none -> 82.8 us  [height_phase(): pl.pallas_call(height_kernel, name='height_phase', out_shape=(jax.ShapeDt...]
    psum x1 -> x0, blocking collectives: 42.2 us -> none  [local_sweep(): gram_two = lax.psum(gram_part, ('a1', 'a2', 'a3')).astype(BF16)]
    dot_general x1 -> x0, local copies, waits for them, and re-layouts: 36.1 us -> none  [local_sweep(): lax.dot_general(time_rows, tensor, (((0,), (0,)), ((), ())), preferred_el...]
    convert_element_type x2 -> x1, other arithmetic: 13.7 us -> 0.01 us  [local_sweep(): u1t = new_time.astype(BF16).T]
  transfers between devices with their start and end apart: 1 -> 0, of which waited for: 0 -> 0; matrix products, arithmetic and copies ran while one was open for 2% -> 0% of each run, Pallas kernels for 0% -> 0%
where the time goes in v3:
time: 793 us; the launch traced here: 792 us
  Pallas kernels  776 us (98%)
  local copies, waits for them, and re-layouts  9.49 us (1%)
    pallas_call x1, Pallas kernels, time_phase(): pl.pallas_call(time_kernel, name='time_phase', out_shape=(jax.ShapeDtypeS...  562 us
    pallas_call x1, Pallas kernels, width_phase(): pl.pallas_call(width_kernel, name='width_phase', out_shape=(jax.ShapeDtyp...  131 us
    pallas_call x1, Pallas kernels, height_phase(): pl.pallas_call(height_kernel, name='height_phase', out_shape=(jax.ShapeDt...  82.8 us

profile of v3, /device:TPU:0, one launch (start us, length us, event | category | flops | bytes accessed | tf_op | source)
XLA Modules:
  0.0 792.1 jit_solution(15213181326853216700)
XLA Ops:
  0.6 0.0 copy-start.4
  0.6 0.0 copy-start.5
  0.7 1.3 dynamic-slice_convert_fusion
  2.0 0.7 pad_maximum_fusion.1.u3t_ref
  2.7 0.0 copy-done.4
  2.7 0.2 copy.27
  2.9 0.7 pad.19.u2p_ref
  3.6 0.0 copy-done.5
  3.6 0.1 copy.28
  3.8 0.7 pad.20.u1_ref
  4.4 562.1 %time_phase.1 = (bf16[2,12,2,384,384]{4,3,2,1,0:T(8,128)(2,1)}, f32[384,48]{1,0:T(8,128)}) custom-call(bf16[69120,720]{1,0:T(8,128)(2,1)} %bitcast.x_hbm, bf16[176,720]{1,0:T(8,128)(2,1)} %pad_maximum_fusion.1.u3t_ref, bf16[2,384,128]{2,1,0:T(8,128)(2,1)} %pad.19.u2p_ref, bf16[384,128]{1,0:T(8,128)(2,1)} %pad.20.u1_ref), custom_call_target="tpu_custom_call" | custom-call | tf_op jit(solution)/shard_map/time_phase/pallas_call | solution.py:222
  566.5 1.0 copy.32
  567.6 0.1 dynamic-slice_bitcast_fusion.5
  567.7 0.6 pad_maximum_fusion.2.u1z_ref
  568.3 0.6 convert_bitcast_fusion.u1t_ref
  568.9 82.8 %height_phase.1 = (f32[720,88]{1,0:T(8,128)}, bf16[24,360,720]{2,1,0:T(8,128)(2,1)}) custom-call(bf16[2,12,2,384,384]{4,3,2,1,0:T(8,128)(2,1)} %get-tuple-element.13.t_hbm, bf16[192,360,720]{2,1,0:T(8,128)(2,1)} %x_hbm.1, bf16[48,384]{1,0:T(8,128)(2,1)} %convert_bitcast_fusion.u1t_ref, bf16[48,192]{1,0:T(8,128)(2,1)} %pad_maximum_fusion.2.u1z_ref, ...), custom_call_target="tpu_custom_call" | custom-call | tf_op jit(solution)/shard_map/height_phase/pallas_call | solution.py:404
  651.7 0.0 copy-done.2
  651.7 0.0 copy-start
  651.7 1.2 copy.33
  653.0 0.0 copy-start.3
  653.0 0.1 dynamic-slice_convert_fusion.1
  653.1 0.6 fusion.2.u2t_ref
  653.8 0.0 copy-done
  653.8 0.1 convert_element_type.32
  653.8 0.3 copy.36
  654.1 0.0 copy-done.3
  654.1 0.1 pad_dynamic-slice_fusion.1
  654.3 0.9 pad_maximum_fusion
  655.2 131.5 %width_phase.1 = (f32[1440,176]{1,0:T(8,128)}, f32[12,88,88]{2,1,0:T(8,128)}, f32[1,1]{1,0:T(1,128)}) custom-call(bf16[24,360,720]{2,1,0:T(8,128)(2,1)} %get-tuple-element.15.z_hbm, bf16[96,360]{1,0:T(8,128)(2,1)} %fusion.2.u2t_ref, bf16[1536,256]{1,0:T(8,128)(2,1)} %bitcast.20), custom_call_target="tpu_custom_call" | custom-call | tf_op jit(solution)/shard_map/width_phase/pallas_call | solution.py:577
  786.7 1.2 reshape.36
  787.9 1.0 copy.35
  788.9 1.4 copy.34
  (8 shorter events, 0.1 us)
Async XLA Ops:
  0.6 2.1 copy-start.4
  0.6 3.0 copy-start.5
  567.6 84.1 %copy-start.2 = (f32[384,48]{0,1:T(8,128)}, f32[384,48]{0,1:T(8,128)S(1)}, u32[]{:S(2)}) copy-start(f32[384,48]{0,1:T(8,128)S(1)} %copy.32) | copy-start | bytes 221188
  651.7 2.1 copy-start
  653.0 1.1 copy-start.3
  786.7 2.2 copy-start.1
